TPU v7x, 32 devices: a whole 2x2x4 slice. The times are simulated.
32 devices in a mesh: dp: 4 (over y, x), seq: 4 (over z), grp: 2 (over core).
Axes of the slice: x: 2, y: 2, z: 4, core: 2. Of those that a mesh axis runs over, the one named last changes fastest.
Arguments:
- text_proj: bfloat16 [3, 16, 12, 128, 128], P(None, 'dp', None, ('seq', 'grp')), may hold values from -50 to 50
- image_proj: bfloat16 [3, 16, 12, 160, 128], P(None, ('dp', 'seq'), None, 'grp'), may hold values from -50 to 50
- text_grad: bfloat16 [16, 12, 128, 128], P('dp', None, ('seq', 'grp')), may hold values from -15 to 15
- image_grad: bfloat16 [16, 12, 160, 128], P(('dp', 'seq'), None, 'grp'), may hold values from -15 to 15
- text_lengths: int32 [16], P(('dp', 'seq')), may hold values from 1 to 128
- norm_gains: float32 [2, 2, 128], replicated, may hold values from 0.7 to 5.2
Outputs:
- text_out: bfloat16 [16, 12, 128, 128], P('dp', None, ('seq', 'grp'))
- image_out: bfloat16 [16, 12, 160, 128], P(('dp', 'seq'), None, 'grp')
- text_proj_grad: bfloat16 [3, 16, 12, 128, 128], P(None, 'dp', None, ('seq', 'grp'))
- image_proj_grad: bfloat16 [3, 16, 12, 160, 128], P(None, ('dp', 'seq'), None, 'grp')
- gain_grad: float32 [2, 2, 128], replicated
All inputs are finite; a program needn't handle non-finite values.
Results may differ from a plain program's by a relative error of at most 0.025.
The roundings to bfloat16 on the way count: a program that leaves them out, or rounds other values in their place, can miss the bound.
Values may be sent and summed in bfloat16 or wider, within the bound.
No kernel may reach another device: no remote copies, remote signals or barrier semaphores. Data moves between devices by JAX's collectives and lax.ppermute only.
A program may use at most 64 MiB of HBM per device.

v0:
```python
import jax
import jax.numpy as jnp
from jax import lax
from jax.sharding import PartitionSpec as P

TXT = 128
EPSILON = 1e-06
MASKED = -1e30


def forward(queries, key_rows, value_rows, key_valid):
    factor = queries.shape[-1] ** (-0.5)
    scores = (
        jnp.einsum("nqd,nkd->nqk", queries, key_rows, preferred_element_type=jnp.float32) * factor
    )
    scores = jnp.where(key_valid[:, None, :], scores, MASKED)
    row_max = jnp.max(scores, axis=-1, keepdims=True)
    exponent = jnp.exp(scores - row_max)
    attn_probs = exponent / jnp.sum(exponent, axis=-1, keepdims=True)
    rounded_probs = attn_probs.astype(jnp.bfloat16)
    attn_local = jnp.einsum(
        "nqk,nkd->nqd", rounded_probs, value_rows, preferred_element_type=jnp.float32
    )
    return (attn_probs, rounded_probs, attn_local)


def backward_terms(queries, key_rows, value_rows, attn_probs, rounded_probs, grad_out):
    factor = queries.shape[-1] ** (-0.5)
    grad_value = jnp.einsum(
        "nqk,nqd->nkd", rounded_probs, grad_out, preferred_element_type=jnp.float32
    )
    grad_probs = jnp.einsum(
        "nqd,nkd->nqk", grad_out, value_rows, preferred_element_type=jnp.float32
    )
    row_delta = jnp.sum(attn_probs * grad_probs, axis=-1, keepdims=True)
    grad_scores = (attn_probs * (grad_probs - row_delta) * factor).astype(jnp.bfloat16)
    grad_query = jnp.einsum(
        "nqk,nkd->nqd", grad_scores, key_rows, preferred_element_type=jnp.float32
    ).astype(jnp.bfloat16)
    grad_key = jnp.einsum("nqk,nqd->nkd", grad_scores, queries, preferred_element_type=jnp.float32)
    return (grad_query, grad_key, grad_value)


def sums_item(packed):
    query_one, key_one, value_one, valid_one, grad_one = packed
    attn_probs, rounded_probs, attn_local = forward(
        query_one[None], key_one[None], value_one[None], valid_one[None]
    )
    grad_query, grad_key, grad_value = backward_terms(
        query_one[None], key_one[None], value_one[None], attn_probs, rounded_probs, grad_one[None]
    )
    return (attn_local[0].astype(jnp.bfloat16), grad_query[0], grad_key[0], grad_value[0])


def whole_item(packed):
    attn_local, grad_query, grad_key, grad_value = sums_item(packed)
    return (attn_local, grad_query, grad_key.astype(jnp.bfloat16), grad_value.astype(jnp.bfloat16))


def unit_parts(raw_bf):
    raw_vals = raw_bf.astype(jnp.float32)
    inverse = lax.rsqrt(jnp.mean(raw_vals * raw_vals, axis=-1, keepdims=True) + EPSILON)
    return (raw_vals * inverse, inverse)


def raw_gradient(grad_normed_bf, unit_vec, inverse, gain_rows):
    grad_normed = grad_normed_bf.astype(jnp.float32)
    gain_part = jnp.sum(grad_normed * unit_vec, axis=(1, 2, 3))
    grad_unit = grad_normed * gain_rows
    grad_raw = inverse * (
        grad_unit - unit_vec * jnp.mean(grad_unit * unit_vec, axis=-1, keepdims=True)
    )
    return (grad_raw.astype(jnp.bfloat16), gain_part)


def global_position(local_row, owner_index, text_rows, text_group, image_rows, grp_count):
    text_place = (
        local_row // text_group * grp_count + owner_index
    ) * text_group + local_row % text_group
    image_place = TXT + owner_index * image_rows + (local_row - text_rows)
    return jnp.where(local_row < text_rows, text_place, image_place)


def per_device(text_proj, image_proj, text_grad, image_grad, text_lengths, norm_gains):
    seq_count = lax.axis_size("seq")
    grp_count = lax.axis_size("grp")
    sample_count, head_count, image_rows, head_size = image_grad.shape
    text_group = text_proj.shape[3]
    text_rows = text_group * seq_count
    local_len = text_rows + image_rows
    text_unit, text_inverse = unit_parts(text_proj[:2])
    image_unit, image_inverse = unit_parts(image_proj[:2])
    text_gain = norm_gains[0][:, None, None, None, :]
    image_gain = norm_gains[1][:, None, None, None, :]
    text_stack = jnp.concatenate(
        [(text_unit * text_gain).astype(jnp.bfloat16), text_proj[2:]], axis=0
    )
    image_stack = jnp.concatenate(
        [(image_unit * image_gain).astype(jnp.bfloat16), image_proj[2:]], axis=0
    )
    text_here, text_cot = (
        lax.all_to_all(text_stack, "seq", split_axis=1, concat_axis=3, tiled=True),
        lax.all_to_all(text_grad[None], "seq", split_axis=1, concat_axis=3, tiled=True),
    )
    joint_rows = jnp.concatenate([text_here, image_stack], axis=3)
    cotangent_rows = jnp.concatenate([text_cot[0], image_grad], axis=2)
    key_row = jnp.arange(local_len * grp_count, dtype=jnp.int32)
    key_place = global_position(
        key_row % local_len, key_row // local_len, text_rows, text_group, image_rows, grp_count
    )
    key_valid = (key_place[None, :] >= TXT) | (key_place[None, :] < text_lengths[:, None])
    full_len = local_len * grp_count
    moved_rows, moved_cot = (
        lax.all_to_all(joint_rows, "grp", split_axis=2, concat_axis=3, tiled=True),
        lax.all_to_all(cotangent_rows[None], "grp", split_axis=2, concat_axis=3, tiled=True),
    )
    head_share = moved_rows.shape[2]
    item_count = sample_count * head_share
    flat_rows = moved_rows.reshape(3, item_count, full_len, head_size)
    item_valid = jnp.broadcast_to(
        key_valid[:, None, :], (sample_count, head_share, full_len)
    ).reshape(item_count, full_len)
    attn_local, grad_query, grad_key, grad_value = lax.map(
        whole_item,
        (
            flat_rows[0],
            flat_rows[1],
            flat_rows[2],
            item_valid,
            moved_cot.reshape(item_count, full_len, head_size),
        ),
    )
    results = jnp.stack([attn_local, grad_query, grad_key, grad_value]).reshape(
        4, sample_count, head_share, full_len, head_size
    )
    placed = lax.all_to_all(results, "grp", split_axis=3, concat_axis=2, tiled=True)
    text_back = lax.all_to_all(
        placed[:, :, :, :text_rows], "seq", split_axis=3, concat_axis=1, tiled=True
    )
    image_back = placed[:, :, :, text_rows:]
    text_raw, text_part = raw_gradient(text_back[1:3], text_unit, text_inverse, text_gain)
    image_raw, image_part = raw_gradient(image_back[1:3], image_unit, image_inverse, image_gain)
    partial_value = jnp.stack([text_part, image_part])
    summed_gain = lax.psum(partial_value, ("dp", "seq", "grp"))
    gain_grad = summed_gain / (sample_count * lax.axis_size("dp") * seq_count)
    text_proj_grad = jnp.concatenate([text_raw, text_back[3:]], axis=0)
    image_proj_grad = jnp.concatenate([image_raw, image_back[3:]], axis=0)
    return (text_back[0], image_back[0], text_proj_grad, image_proj_grad, gain_grad)


def solution(mesh):
    placed = (
        P(None, "dp", None, ("seq", "grp"), None),
        P(None, ("dp", "seq"), None, "grp", None),
        P("dp", None, ("seq", "grp"), None),
        P(("dp", "seq"), None, "grp", None),
        P(("dp", "seq")),
        P(),
    )
    return jax.shard_map(
        per_device,
        mesh=mesh,
        in_specs=placed,
        out_specs=(
            P("dp", None, ("seq", "grp"), None),
            P(("dp", "seq"), None, "grp", None),
            P(None, "dp", None, ("seq", "grp"), None),
            P(None, ("dp", "seq"), None, "grp", None),
            P(),
        ),
        check_vma=False,
    )
```

profile of v0, /device:TPU:10, one launch (start us, length us, event | category | flops | bytes accessed | tf_op | source)
XLA Modules:
  0.0 161.8 jit_solution(1333477667918705269)
XLA Ops:
  0.6 5.5 %all-to-all-start.2 = ((bf16[1,4,12,16,128]{4,3,2,0,1:T(8,128)(2,1)}), bf16[1,4,12,16,128]{4,3,2,0,1:T(8,128)(2,1)S(1)}, u32[]{:S(2)}, u32[]{:S(2)}) async-start(bf16[1,4,12,16,128]{4,3,2,0,1:T(8,128)(2,1)} %bitcast.157), calls=%async_computation.2 | async-start | bytes 393216 | tf_op jit(solution)/shard_map/all_to_all | solution.py:103
  6.8 1.3 fusion.56
  8.1 1.3 fusion.54
  10.2 1.0 copy.85
  12.1 4.1 %all_to_all.96 = bf16[1,1,12,144,128]{4,3,1,0,2:T(8,128)(2,1)S(1)} all-to-all(bf16[1,1,12,144,128]{4,3,1,0,2:T(8,128)(2,1)S(1)} %maximum_bitcast_fusion.1), channel_id=1, replica_groups=mesh['dp'=4,'seq'=4,'grp'=2] {'grp'}, dimensions={2} | all-to-all | bytes 884736 | tf_op jit(solution)/shard_map/all_to_all | solution.py:115
  16.2 5.0 %all-to-all-start = ((bf16[3,4,12,16,128]{4,3,2,0,1:T(8,128)(2,1)}), bf16[3,4,12,16,128]{4,3,2,0,1:T(8,128)(2,1)S(1)}, u32[]{:S(2)}, u32[]{:S(2)}) async-start(bf16[3,4,12,16,128]{4,3,2,0,1:T(8,128)(2,1)} %copy.85), calls=%async_computation | async-start | bytes 1179648 | tf_op jit(solution)/shard_map/all_to_all | solution.py:102
  23.0 11.4 %all-to-all-done = bf16[3,4,12,16,128]{4,3,2,0,1:T(8,128)(2,1)S(1)} async-done(((bf16[3,4,12,16,128]{4,3,2,0,1:T(8,128)(2,1)}), bf16[3,4,12,16,128]{4,3,2,0,1:T(8,128)(2,1)S(1)}, u32[]{:S(2)}, u32[]{:S(2)}) %all-to-all-start) | async-done | bytes 589856 | tf_op jit(solution)/shard_map/all_to_all | solution.py:102
  34.7 4.8 %all_to_all.97 = bf16[3,1,12,144,128]{4,3,1,0,2:T(8,128)(2,1)S(1)} all-to-all(bf16[3,1,12,144,128]{4,3,1,0,2:T(8,128)(2,1)S(1)} %maximum_maximum_fusion), channel_id=1, replica_groups=mesh['dp'=4,'seq'=4,'grp'=2] {'grp'}, dimensions={2} | all-to-all | bytes 2654208 | tf_op jit(solution)/shard_map/all_to_all | solution.py:114
  40.6 32.7 %while.16 = (s32[]{:T(128)}, bf16[6,288,128]{2,1,0:T(8,128)(2,1)}, bf16[6,288,128]{2,1,0:T(8,128)(2,1)}, bf16[6,288,128]{2,1,0:T(8,128)(2,1)}, bf16[6,288,128]{2...) while((s32[]{:T(128)}, bf16[6,288,128]{2,1,0:T(8,128)(2,1)}, ...), condition=%wide.region_6.7_spmd, body=%wide.region_2.6_spmd.sunk | while | flops 129290400 | bytes 4506681 | solution.py:123
  40.9 1.1 fusion.116
  42.1 0.9 fusion.113
  43.0 1.1 multiply_reduce_fusion.2
  46.4 1.1 fusion.116
  48.4 1.1 multiply_reduce_fusion.2
  51.8 1.1 fusion.116
  53.0 0.9 fusion.113
  53.9 1.1 multiply_reduce_fusion.2
  57.3 1.1 fusion.116
  59.3 1.1 multiply_reduce_fusion.2
  62.7 1.1 fusion.116
  64.8 1.1 multiply_reduce_fusion.2
  68.2 1.1 fusion.116
  70.2 1.1 multiply_reduce_fusion.2
  73.3 1.5 maximum_bitcast_fusion
  74.8 1.4 copy.95
  76.1 5.2 %all_to_all.98 = bf16[4,1,6,288,128]{4,0,2,1,3:T(4,128)(2,1)S(1)} all-to-all(bf16[4,1,6,288,128]{4,0,2,1,3:T(4,128)(2,1)S(1)} %copy.95), channel_id=1, replica_groups=mesh['dp'=4,'seq'=4,'grp'=2] {'grp'}, dimensions={3} | all-to-all | bytes 3538944 | tf_op jit(solution)/shard_map/all_to_all | solution.py:136
  81.7 1.6 copy.97
  83.3 7.5 %all-to-all-start.5 = ((bf16[4,1,12,64,128]{4,2,1,0,3:T(8,128)(2,1)}), bf16[4,1,12,64,128]{4,2,1,0,3:T(8,128)(2,1)}, u32[]{:S(2)}, u32[]{:S(2)}) async-start(bf16[4,1,12,64,128]{4,2,1,0,3:T(8,128)(2,1)} %copy.97), calls=%async_computation.5 | async-start | bytes 2097152 | tf_op jit(solution)/shard_map/all_to_all | solution.py:137
  94.0 19.8 %all-to-all-done.5 = bf16[4,1,12,64,128]{4,2,1,0,3:T(8,128)(2,1)} async-done(((bf16[4,1,12,64,128]{4,2,1,0,3:T(8,128)(2,1)}), bf16[4,1,12,64,128]{4,2,1,0,3:T(8,128)(2,1)}, u32[]{:S(2)}, u32[]{:S(2)}) %all-to-all-start.5) | async-done | bytes 786464 | tf_op jit(solution)/shard_map/all_to_all | solution.py:137
  113.8 1.7 %copy.98 = bf16[4,1,12,64,128]{4,3,2,0,1:T(8,128)(2,1)S(1)} copy(bf16[4,1,12,64,128]{4,2,1,0,3:T(8,128)(2,1)} %all-to-all-done.5) | data formatting | bytes 1572864 | tf_op jit(solution)/shard_map/all_to_all | solution.py:137
  116.1 42.8 %psum.7 = f32[2,2,128]{2,1,0:T(2,128)S(1)} all-reduce(f32[2,2,128]{2,1,0:T(2,128)S(1)} %pad_maximum_fusion.3), channel_id=1, replica_groups=mesh['dp'=4,'seq'=4,'grp'=2] {'dp','seq','grp'}, use_global_device_ids=true, to_apply=%region_11.12 | all-reduce | flops 512 | bytes 4096 | tf_op jit(solution)/shard_map/psum | solution.py:144
  160.1 1.0 copy.100
  (87 shorter events, 28.0 us)
Async XLA Ops:
  0.6 9.5 %copy-start.1 = (bf16[3,4,12,16,128]{4,3,2,1,0:T(8,128)(2,1)S(1)}, bf16[3,4,12,16,128]{4,3,2,1,0:T(8,128)(2,1)}, u32[]{:S(2)}) copy-start(bf16[3,4,12,16,128]{4,3,2,1,0:T(8,128)(2,1)} %param.8) | copy-start | bytes 1769476
  0.6 11.4 %all-to-all-start.2 = ((bf16[1,4,12,16,128]{4,3,2,0,1:T(8,128)(2,1)}), bf16[1,4,12,16,128]{4,3,2,0,1:T(8,128)(2,1)S(1)}, u32[]{:S(2)}, u32[]{:S(2)}) async-start(bf16[1,4,12,16,128]{4,3,2,0,1:T(8,128)(2,1)} %bitcast.157), calls=%async_computation.2 | async-start | bytes 393216 | tf_op jit(solution)/shard_map/all_to_all | solution.py:103
  8.1 4.0 %copy-start.3 = (bf16[1,12,80,128]{3,2,1,0:T(8,128)(2,1)S(1)}, bf16[1,12,80,128]{3,2,1,0:T(8,128)(2,1)}, u32[]{:S(2)}) copy-start(bf16[1,12,80,128]{3,2,1,0:T(8,128)(2,1)} %param.11) | copy-start | bytes 737284
  11.2 10.1 %copy-start = (bf16[3,1,12,80,128]{4,3,2,1,0:T(8,128)(2,1)S(1)}, bf16[3,1,12,80,128]{4,3,2,1,0:T(8,128)(2,1)}, u32[]{:S(2)}) copy-start(bf16[3,1,12,80,128]{4,3,2,1,0:T(8,128)(2,1)} %param.9) | copy-start | bytes 2211844
  16.2 18.2 %all-to-all-start = ((bf16[3,4,12,16,128]{4,3,2,0,1:T(8,128)(2,1)}), bf16[3,4,12,16,128]{4,3,2,0,1:T(8,128)(2,1)S(1)}, u32[]{:S(2)}, u32[]{:S(2)}) async-start(bf16[3,4,12,16,128]{4,3,2,0,1:T(8,128)(2,1)} %copy.85), calls=%async_computation | async-start | bytes 1179648 | tf_op jit(solution)/shard_map/all_to_all | solution.py:102
  39.5 1.0 copy-start.2
  83.3 30.5 %all-to-all-start.5 = ((bf16[4,1,12,64,128]{4,2,1,0,3:T(8,128)(2,1)}), bf16[4,1,12,64,128]{4,2,1,0,3:T(8,128)(2,1)}, u32[]{:S(2)}, u32[]{:S(2)}) async-start(bf16[4,1,12,64,128]{4,2,1,0,3:T(8,128)(2,1)} %copy.97), calls=%async_computation.5 | async-start | bytes 2097152 | tf_op jit(solution)/shard_map/all_to_all | solution.py:137
where the time goes:
time: 163 us; the launch traced here: 162 us
  blocking collectives  56.9 us (35%)
  waiting for transfers between devices  32.1 us (20%)
  matrix products  31 us (19%)
  starting transfers between devices  17.9 us (11%)
  local copies, waits for them, and re-layouts  12.2 us (7%)
  other arithmetic  9.94 us (6%)
    psum x1, blocking collectives, per_device(): summed_gain = lax.psum(partial_value, ('dp', 'seq', 'grp'))  42.8 us
    all_to_all x1, waiting for transfers between devices, per_device(): lax.all_to_all(placed[:, :, :, :text_rows], 'seq', split_axis=3, concat_a...  19.8 us
    all_to_all x1, waiting for transfers between devices, per_device(): lax.all_to_all(text_stack, 'seq', split_axis=1, concat_axis=3, tiled=True)  11.4 us
    all_to_all x1, starting transfers between devices, per_device(): lax.all_to_all(placed[:, :, :, :text_rows], 'seq', split_axis=3, concat_a...  7.47 us
    dot_general x6, matrix products, backward_terms(): jnp.einsum('nqk,nqd->nkd', rounded_probs, grad_out, preferred_element_typ...  6.74 us
    dot_general x6, matrix products, backward_terms(): jnp.einsum('nqd,nkd->nqk', grad_out, value_rows, preferred_element_type=j...  6.74 us
    dot_general x6, matrix products, forward(): jnp.einsum('nqk,nkd->nqd', rounded_probs, value_rows, preferred_element_t...  5.55 us
    all_to_all x1, starting transfers between devices, per_device(): lax.all_to_all(text_grad[None], 'seq', split_axis=1, concat_axis=3, tiled...  5.46 us
  transfers between devices with their start and end apart: 3, of which 3 were waited for; matrix products, arithmetic and copies ran while one was open for 6% of the time, Pallas kernels for 0%

commit v1 on v0

--- a/solution.py
+++ b/solution.py
@@ -6,6 +6,30 @@
 TXT = 128
 EPSILON = 1e-06
 MASKED = -1e30
+
+
+def cut_along(x, dim, peers):
+    shape = x.shape
+    blocks = x.reshape(*shape[:dim], peers, shape[dim] // peers, *shape[dim + 1 :])
+    return jnp.moveaxis(blocks, dim, 0)
+
+
+def laid_out(pieces, dim):
+    pieces = jnp.moveaxis(pieces, 0, dim)
+    dims = pieces.shape
+    return pieces.reshape(*dims[:dim], dims[dim] * dims[dim + 1], *dims[dim + 2 :])
+
+
+def sent_to_each(shard, axis, split_dim, concat_dim):
+    length, index = (lax.axis_size(axis), lax.axis_index(axis))
+    tiles = cut_along(shard, split_dim, length)
+    result = tiles
+    for step in range(1, length):
+        target, source = ((index + step) % length, (index - step) % length)
+        sent = lax.dynamic_index_in_dim(tiles, target, 0)
+        other = lax.ppermute(sent, axis, [(i, (i + step) % length) for i in range(length)])
+        result = lax.dynamic_update_slice_in_dim(result, other, source, axis=0)
+    return laid_out(result, concat_dim)
 
 
 def forward(queries, key_rows, value_rows, key_valid):
@@ -99,7 +123,7 @@
         [(image_unit * image_gain).astype(jnp.bfloat16), image_proj[2:]], axis=0
     )
     text_here, text_cot = (
-        lax.all_to_all(text_stack, "seq", split_axis=1, concat_axis=3, tiled=True),
+        sent_to_each(text_stack, "seq", 1, 3),
         lax.all_to_all(text_grad[None], "seq", split_axis=1, concat_axis=3, tiled=True),
     )
     joint_rows = jnp.concatenate([text_here, image_stack], axis=3)

time: 163 us -> 145 us (0.89)
  matrix products: 31 us -> 17 us
  local copies, waits for them, and re-layouts: 12.2 us -> 9.03 us
  waiting for transfers between devices: 32.1 us -> 30 us
  other arithmetic: 9.94 us -> 11.9 us
    all_to_all x1 -> x0, waiting for transfers between devices: 11.4 us -> none  [per_device(): lax.all_to_all(text_stack, 'seq', split_axis=1, concat_axis=3, tiled=True)]
    ppermute x0 -> x3, starting transfers between devices: none -> 6.47 us  [sent_to_each(): lax.ppermute(sent, axis, [(i, (i + step) % length) for i in range(length)])]
    ppermute x0 -> x3, waiting for transfers between devices: none -> 5.62 us  [sent_to_each(): lax.ppermute(sent, axis, [(i, (i + step) % length) for i in range(length)])]
    dot_general x6, matrix products: 6.74 us -> 1.47 us  [backward_terms(): jnp.einsum('nqk,nqd->nkd', rounded_probs, grad_out, preferred_element_typ...]
    dot_general x6, matrix products: 6.74 us -> 1.5 us  [backward_terms(): jnp.einsum('nqd,nkd->nqk', grad_out, value_rows, preferred_element_type=j...]
    all_to_all x1, waiting for transfers between devices: 0.88 us -> 5.97 us  [per_device(): lax.all_to_all(text_grad[None], 'seq', split_axis=1, concat_axis=3, tiled...]
    all_to_all x1 -> x0, starting transfers between devices: 5 us -> none  [per_device(): lax.all_to_all(text_stack, 'seq', split_axis=1, concat_axis=3, tiled=True)]
    dot_general x6, matrix products: 5.13 us -> 1.44 us  [backward_terms(): jnp.einsum('nqk,nqd->nkd', grad_scores, queries, preferred_element_type=j...]
  transfers between devices with their start and end apart: 3 -> 5, of which waited for: 3 -> 4; matrix products, arithmetic and copies ran while one was open for 6% -> 4% of each run, Pallas kernels for 0% -> 0%
where the time goes in v1:
time: 145 us; the launch traced here: 144 us
  blocking collectives  56.7 us (39%)
  waiting for transfers between devices  30 us (21%)
  starting transfers between devices  17.6 us (12%)
  matrix products  17 us (12%)
  other arithmetic  11.9 us (8%)
  local copies, waits for them, and re-layouts  9.03 us (6%)
  between operations  1.77 us (1%)
    psum x1, blocking collectives, per_device(): summed_gain = lax.psum(partial_value, ('dp', 'seq', 'grp'))  42.7 us
    all_to_all x1, waiting for transfers between devices, per_device(): lax.all_to_all(placed[:, :, :, :text_rows], 'seq', split_axis=3, concat_a...  18.4 us
    ppermute x3, starting transfers between devices, sent_to_each(): lax.ppermute(sent, axis, [(i, (i + step) % length) for i in range(length)])  6.47 us
    all_to_all x1, starting transfers between devices, per_device(): lax.all_to_all(text_grad[None], 'seq', split_axis=1, concat_axis=3, tiled...  6.11 us
    all_to_all x1, waiting for transfers between devices, per_device(): lax.all_to_all(text_grad[None], 'seq', split_axis=1, concat_axis=3, tiled...  5.97 us
    ppermute x3, waiting for transfers between devices, sent_to_each(): lax.ppermute(sent, axis, [(i, (i + step) % length) for i in range(length)])  5.62 us
    dot_general x6, matrix products, forward(): jnp.einsum('nqk,nkd->nqd', rounded_probs, value_rows, preferred_element_t...  5.55 us
    dot_general x6, matrix products, backward_terms(): jnp.einsum('nqk,nkd->nqd', grad_scores, key_rows, preferred_element_type=...  5.53 us
  transfers between devices with their start and end apart: 5, of which 4 were waited for; matrix products, arithmetic and copies ran while one was open for 4% of the time, Pallas kernels for 0%

profile of v1, /device:TPU:10, one launch (start us, length us, event | category | flops | bytes accessed | tf_op | source)
XLA Modules:
  0.0 144.1 jit_solution(8158529448860911546)
XLA Ops:
  0.7 1.3 fusion.56
  2.0 0.9 slice.62
  3.7 1.3 fusion.54
  5.6 1.6 %collective-permute-start = (bf16[1,3,1,12,16,128]{5,4,3,0,1,2:T(8,128)(2,1)S(1)}, bf16[1,3,1,12,16,128]{5,4,3,0,1,2:T(8,128)(2,1)S(1)}, u32[]{:S(2)}, u32[]{:S(2)}) collective-permute-start(bf16[1,3,1,12,16,128]{5,4,3,0,1,2:T(8,128)(2,1)S(1)} %get-tuple-element.120), channel_id=1, source_target_pairs={{0,2},{2,4},{4,6},{6,0},{1,3},{3,5},{5,7},{7,1},{8,10},{10,12},{12... | collective-permute-start | bytes 442376 | tf_op jit(solution)/shard_map/ppermute | solution.py:30
  7.2 4.4 %collective-permute-start.1 = (bf16[1,3,1,12,16,128]{5,4,3,0,1,2:T(8,128)(2,1)S(1)}, bf16[1,3,1,12,16,128]{5,4,3,0,1,2:T(8,128)(2,1)S(1)}, u32[]{:S(2)}, u32[]{:S(2)}) collective-permute-start(bf16[1,3,1,12,16,128]{5,4,3,0,1,2:T(8,128)(2,1)S(1)} %get-tuple-element.121), channel_id=1, source_target_pairs={{0,4},{2,6},{4,0},{6,2},{1,5},{3,7},{5,1},{7,3},{8,12},{10,14},{12... | collective-permute-start | bytes 442376 | tf_op jit(solution)/shard_map/ppermute | solution.py:30
  13.8 3.2 %collective-permute-done = bf16[1,3,1,12,16,128]{5,4,3,0,1,2:T(8,128)(2,1)S(1)} collective-permute-done((bf16[1,3,1,12,16,128]{5,4,3,0,1,2:T(8,128)(2,1)S(1)}, bf16[1,3,1,12,16,128]{5,4,3,0,1,2:T(8,128)(2,1)S(1)}, u32[]{:S(2)}, u32[]{:S(2)}) %collective-permute-start) | collective-permute-done | bytes 147488 | tf_op jit(solution)/shard_map/ppermute | solution.py:30
  17.1 2.4 %collective-permute-done.1 = bf16[1,3,1,12,16,128]{5,4,3,0,1,2:T(8,128)(2,1)S(1)} collective-permute-done((bf16[1,3,1,12,16,128]{5,4,3,0,1,2:T(8,128)(2,1)S(1)}, bf16[1,3,1,12,16,128]{5,4,3,0,1,2:T(8,128)(2,1)S(1)}, u32[]{:S(2)}, u32[]{:S(2)}) %collective-permute-start.1) | collective-permute-done | bytes 147488 | tf_op jit(solution)/shard_map/ppermute | solution.py:30
  19.8 4.8 %all_to_all.78 = bf16[3,1,12,144,128]{4,3,1,0,2:T(8,128)(2,1)S(1)} all-to-all(bf16[3,1,12,144,128]{4,3,1,0,2:T(8,128)(2,1)S(1)} %maximum_maximum_fusion), channel_id=1, replica_groups=mesh['dp'=4,'seq'=4,'grp'=2] {'grp'}, dimensions={2} | all-to-all | bytes 2654208 | tf_op jit(solution)/shard_map/all_to_all | solution.py:138
  24.6 6.1 %all-to-all-start.1 = ((bf16[1,4,12,16,128]{4,3,2,0,1:T(8,128)(2,1)}), bf16[1,4,12,16,128]{4,3,2,0,1:T(8,128)(2,1)S(1)}, u32[]{:S(2)}, u32[]{:S(2)}) async-start(bf16[1,4,12,16,128]{4,3,2,0,1:T(8,128)(2,1)} %bitcast.24), calls=%async_computation.1 | async-start | bytes 393216 | tf_op jit(solution)/shard_map/all_to_all | solution.py:127
  31.0 6.0 %all-to-all-done.1 = bf16[1,4,12,16,128]{4,3,2,0,1:T(8,128)(2,1)S(1)} async-done(((bf16[1,4,12,16,128]{4,3,2,0,1:T(8,128)(2,1)}), bf16[1,4,12,16,128]{4,3,2,0,1:T(8,128)(2,1)S(1)}, u32[]{:S(2)}, u32[]{:S(2)}) %all-to-all-start.1) | async-done | bytes 196640 | tf_op jit(solution)/shard_map/all_to_all | solution.py:127
  37.0 4.1 %all_to_all.79 = bf16[1,1,12,144,128]{4,3,1,0,2:T(8,128)(2,1)S(1)} all-to-all(bf16[1,1,12,144,128]{4,3,1,0,2:T(8,128)(2,1)S(1)} %maximum_bitcast_fusion.1), channel_id=1, replica_groups=mesh['dp'=4,'seq'=4,'grp'=2] {'grp'}, dimensions={2} | all-to-all | bytes 884736 | tf_op jit(solution)/shard_map/all_to_all | solution.py:139
  41.1 18.7 %while.16 = (s32[]{:T(128)}, bf16[6,288,128]{2,1,0:T(8,128)(2,1)}, bf16[6,288,128]{2,1,0:T(8,128)(2,1)}, bf16[6,288,128]{2,1,0:T(8,128)(2,1)S(1)}, bf16[6,288,12...) while((s32[]{:T(128)}, bf16[6,288,128]{2,1,0:T(8,128)(2,1)}, ...), condition=%wide.region_6.7_spmd, body=%wide.region_2.6_spmd.sunk | while | flops 129290400 | bytes 4506681 | solution.py:147
  41.8 0.9 fusion.112
  43.3 0.9 fusion.113
  44.9 0.9 fusion.112
  46.4 0.9 fusion.113
  48.0 0.9 fusion.112
  49.5 0.9 fusion.113
  51.1 0.9 fusion.112
  52.6 0.9 fusion.113
  54.2 0.9 fusion.112
  55.8 0.9 fusion.113
  57.3 0.9 fusion.112
  58.9 0.9 fusion.113
  59.8 1.4 maximum_bitcast_fusion
  61.2 1.4 copy.74
  62.5 5.2 %all_to_all.80 = bf16[4,1,6,288,128]{4,0,2,1,3:T(4,128)(2,1)S(1)} all-to-all(bf16[4,1,6,288,128]{4,0,2,1,3:T(4,128)(2,1)S(1)} %copy.74), channel_id=1, replica_groups=mesh['dp'=4,'seq'=4,'grp'=2] {'grp'}, dimensions={3} | all-to-all | bytes 3538944 | tf_op jit(solution)/shard_map/all_to_all | solution.py:160
  68.1 1.5 %copy.76 = bf16[4,1,12,64,128]{4,2,1,0,3:T(8,128)(2,1)} copy(bf16[4,1,12,64,128]{4,3,1,0,2:T(8,128)(2,1)S(1)} %slice.80) | data formatting | bytes 1572864 | tf_op jit(solution)/shard_map/slice | solution.py:162
  69.6 5.0 %all-to-all-start.4 = ((bf16[4,1,12,64,128]{4,2,1,0,3:T(8,128)(2,1)}), bf16[4,1,12,64,128]{4,2,1,0,3:T(8,128)(2,1)S(1)}, u32[]{:S(2)}, u32[]{:S(2)}) async-start(bf16[4,1,12,64,128]{4,2,1,0,3:T(8,128)(2,1)} %copy.76), calls=%async_computation.4 | async-start | bytes 2097152 | tf_op jit(solution)/shard_map/all_to_all | solution.py:161
  74.6 2.2 %fusion.47 = (f32[2,128]{1,0:T(2,128)}, f32[2,12,80]{2,0,1:T(2,128)S(1)}) fusion(f32[2,12,80]{2,0,1:T(2,128)} %copy-done.5, bf16[4,1,12,144,128]{4,3,1,0,2:T(8,128)(2,1)S(1)} %bitcast.144, f32[2,128]{1,0:T(2,128)} %copy-done.9, bf16[3,1,12,80,128]{4,3,2,1,0:T(8,128)(2,1)S(1)} %copy-done), kind=kLoop, calls=%fused_computation.60 | loop fusion | flops 1963904 | bytes 1000448 | tf_op jit(solution)/shard_map/reduce_sum | solution.py:92
  79.3 18.4 %all-to-all-done.4 = bf16[4,1,12,64,128]{4,2,1,0,3:T(8,128)(2,1)S(1)} async-done(((bf16[4,1,12,64,128]{4,2,1,0,3:T(8,128)(2,1)}), bf16[4,1,12,64,128]{4,2,1,0,3:T(8,128)(2,1)S(1)}, u32[]{:S(2)}, u32[]{:S(2)}) %all-to-all-start.4) | async-done | bytes 786464 | tf_op jit(solution)/shard_map/all_to_all | solution.py:161
  99.4 42.7 %psum.7 = f32[2,2,128]{2,1,0:T(2,128)S(1)} all-reduce(f32[2,2,128]{2,1,0:T(2,128)S(1)} %pad_maximum_fusion.3), channel_id=1, replica_groups=mesh['dp'=4,'seq'=4,'grp'=2] {'dp','seq','grp'}, use_global_device_ids=true, to_apply=%region_11.12 | all-reduce | flops 512 | bytes 4096 | tf_op jit(solution)/shard_map/psum | solution.py:168
  (109 shorter events, 17.3 us)
Async XLA Ops:
  0.6 10.9 %copy-start = (bf16[3,1,12,80,128]{4,3,2,1,0:T(8,128)(2,1)S(1)}, bf16[3,1,12,80,128]{4,3,2,1,0:T(8,128)(2,1)}, u32[]{:S(2)}) copy-start(bf16[3,1,12,80,128]{4,3,2,1,0:T(8,128)(2,1)} %param.9) | copy-start | bytes 2211844
  3.7 8.4 %copy-start.9 = (f32[2,128]{1,0:T(2,128)}, f32[2,128]{1,0:T(2,128)S(1)}, u32[]{:S(2)}) copy-start(f32[2,128]{1,0:T(2,128)S(1)} %get-tuple-element.123) | copy-start | bytes 3076
  3.7 9.3 %copy-start.7 = (f32[2,128]{1,0:T(2,128)}, f32[2,128]{1,0:T(2,128)S(1)}, u32[]{:S(2)}) copy-start(f32[2,128]{1,0:T(2,128)S(1)} %get-tuple-element.122) | copy-start | bytes 3076
  3.7 9.3 %copy-start.2 = (f32[2,4,12,16]{3,2,1,0:T(8,128)}, f32[2,4,12,16]{3,2,1,0:T(8,128)S(1)}, u32[]{:S(2)}) copy-start(f32[2,4,12,16]{3,2,1,0:T(8,128)S(1)} %add_rsqrt_fusion) | copy-start | bytes 18436
  5.1 14.4 %collective-permute-start.2 = (bf16[1,3,1,12,16,128]{5,4,3,0,1,2:T(8,128)(2,1)S(1)}, bf16[1,3,1,12,16,128]{5,4,3,0,1,2:T(8,128)(2,1)S(1)}, u32[]{:S(2)}, u32[]{:S(2)}) collective-permute-start(bf16[1,3,1,12,16,128]{5,4,3,0,1,2:T(8,128)(2,1)S(1)} %get-tuple-element.119), channel_id=1, source_target_pairs={{0,6},{2,0},{4,2},{6,4},{1,7},{3,1},{5,3},{7,5},{8,14},{10,8},{12,... | collective-permute-start | bytes 442376 | tf_op jit(solution)/shard_map/ppermute | solution.py:30
  5.6 11.5 %collective-permute-start = (bf16[1,3,1,12,16,128]{5,4,3,0,1,2:T(8,128)(2,1)S(1)}, bf16[1,3,1,12,16,128]{5,4,3,0,1,2:T(8,128)(2,1)S(1)}, u32[]{:S(2)}, u32[]{:S(2)}) collective-permute-start(bf16[1,3,1,12,16,128]{5,4,3,0,1,2:T(8,128)(2,1)S(1)} %get-tuple-element.120), channel_id=1, source_target_pairs={{0,2},{2,4},{4,6},{6,0},{1,3},{3,5},{5,7},{7,1},{8,10},{10,12},{12... | collective-permute-start | bytes 442376 | tf_op jit(solution)/shard_map/ppermute | solution.py:30
  7.2 12.3 %collective-permute-start.1 = (bf16[1,3,1,12,16,128]{5,4,3,0,1,2:T(8,128)(2,1)S(1)}, bf16[1,3,1,12,16,128]{5,4,3,0,1,2:T(8,128)(2,1)S(1)}, u32[]{:S(2)}, u32[]{:S(2)}) collective-permute-start(bf16[1,3,1,12,16,128]{5,4,3,0,1,2:T(8,128)(2,1)S(1)} %get-tuple-element.121), channel_id=1, source_target_pairs={{0,4},{2,6},{4,0},{6,2},{1,5},{3,7},{5,1},{7,3},{8,12},{10,14},{12... | collective-permute-start | bytes 442376 | tf_op jit(solution)/shard_map/ppermute | solution.py:30
  12.1 0.6 copy-start.5
  24.6 12.4 %all-to-all-start.1 = ((bf16[1,4,12,16,128]{4,3,2,0,1:T(8,128)(2,1)}), bf16[1,4,12,16,128]{4,3,2,0,1:T(8,128)(2,1)S(1)}, u32[]{:S(2)}, u32[]{:S(2)}) async-start(bf16[1,4,12,16,128]{4,3,2,0,1:T(8,128)(2,1)} %bitcast.24), calls=%async_computation.1 | async-start | bytes 393216 | tf_op jit(solution)/shard_map/all_to_all | solution.py:127
  30.8 6.1 %copy-start.4 = (bf16[1,12,80,128]{3,2,1,0:T(8,128)(2,1)S(1)}, bf16[1,12,80,128]{3,2,1,0:T(8,128)(2,1)}, u32[]{:S(2)}) copy-start(bf16[1,12,80,128]{3,2,1,0:T(8,128)(2,1)} %param.11) | copy-start | bytes 737284
  69.6 28.0 %all-to-all-start.4 = ((bf16[4,1,12,64,128]{4,2,1,0,3:T(8,128)(2,1)}), bf16[4,1,12,64,128]{4,2,1,0,3:T(8,128)(2,1)S(1)}, u32[]{:S(2)}, u32[]{:S(2)}) async-start(bf16[4,1,12,64,128]{4,2,1,0,3:T(8,128)(2,1)} %copy.76), calls=%async_computation.4 | async-start | bytes 2097152 | tf_op jit(solution)/shard_map/all_to_all | solution.py:161
  74.6 2.9 %copy-start.6 = (f32[2,12,80]{2,0,1:T(2,128)S(1)}, f32[2,12,80]{2,0,1:T(2,128)}, u32[]{:S(2)}) copy-start(f32[2,12,80]{2,0,1:T(2,128)} %copy-done.5) | copy-start | bytes 23044
  74.6 2.9 %copy-start.10 = (f32[2,128]{1,0:T(2,128)S(1)}, f32[2,128]{1,0:T(2,128)}, u32[]{:S(2)}) copy-start(f32[2,128]{1,0:T(2,128)} %copy-done.9) | copy-start | bytes 3076
  78.3 19.9 %copy-start.1 = (bf16[3,4,12,16,128]{4,3,2,1,0:T(8,128)(2,1)S(1)}, bf16[3,4,12,16,128]{4,3,2,1,0:T(8,128)(2,1)}, u32[]{:S(2)}) copy-start(bf16[3,4,12,16,128]{4,3,2,1,0:T(8,128)(2,1)} %param.8) | copy-start | bytes 1769476
  78.3 19.9 %copy-start.3 = (f32[2,4,12,16]{3,2,1,0:T(8,128)S(1)}, f32[2,4,12,16]{3,2,1,0:T(8,128)}, u32[]{:S(2)}) copy-start(f32[2,4,12,16]{3,2,1,0:T(8,128)} %copy-done.2) | copy-start | bytes 18436
  78.3 19.9 %copy-start.8 = (f32[2,128]{1,0:T(2,128)S(1)}, f32[2,128]{1,0:T(2,128)}, u32[]{:S(2)}) copy-start(f32[2,128]{1,0:T(2,128)} %copy-done.7) | copy-start | bytes 3076
  97.7 1.8 %copy-start.11 = (f32[2,128]{1,0:T(2,128)S(1)}, f32[2,128]{1,0:T(2,128)}, u32[]{:S(2)}) copy-start(f32[2,128]{1,0:T(2,128)} %get-tuple-element.84) | copy-start | bytes 3076
